TPU v7x, 16 devices: a 4x2x1 block of a 4x4x8 slice. The times are simulated.
16 devices in a mesh: dp: 2 (over y, z), tp: 8 (over x, core).
Axes of the slice: x: 4, y: 2, z: 1, core: 2. Of those that a mesh axis runs over, the one named last changes fastest.
The devices are a block of a 4x4x8 slice.
Arguments:
- X: bfloat16 [8192, 4096], P('dp'), parts along dimension 0
- W: bfloat16 [4096, 32768], P(None, 'tp')
- labels: int32 [8192], P('dp'), parts along dimension 0
Outputs:
- output 1: float32 [2], P('dp'), parts along dimension 0
- output 2: bfloat16 [8192, 32768], P('dp', 'tp'), parts along dimension 0
- output 3: bfloat16 [8192, 4096], P('dp'), parts along dimension 0
There are 2 independent parts. A program takes and returns all parts, laid end to end along the dimension named above; an argument that names none is the same for every part.
All inputs are finite; a program needn't handle non-finite values.
Results may differ from a plain program's by a relative error of at most 0.001.
Values are sent between devices in bfloat16 or wider.
A program may use at most 768 MiB of HBM per device.

v0:
```python
import jax
import jax.numpy as jnp
from jax import lax
from jax.sharding import PartitionSpec as P


def solution(mesh):
    def local(X, W, labels):
        T = X.shape[0]
        Vl = W.shape[1]
        off = lax.axis_index('tp') * Vl
        Z = jnp.dot(X, W, preferred_element_type=jnp.float32)
        m = Z.max(axis=1)
        s = jnp.exp(Z - m[:, None]).sum(axis=1)
        hit = jnp.arange(Vl, dtype=jnp.int32)[None, :] == (labels - off)[:, None]
        z = jnp.where(hit, Z, 0.0).sum(axis=1)
        M = lax.pmax(m, 'tp')
        st = lax.psum(jnp.stack([s * jnp.exp(m - M), z]), 'tp')
        S, zt = st[0], st[1]
        L = jnp.mean(M + jnp.log(S) - zt).reshape(1)
        G = ((jnp.exp(Z - M[:, None]) / S[:, None] - hit.astype(jnp.float32)) / T).astype(jnp.bfloat16)
        dW = jnp.einsum('th,tv->hv', X, G, preferred_element_type=jnp.float32).astype(jnp.bfloat16)
        dXp = jnp.einsum('tv,hv->th', G, W, preferred_element_type=jnp.float32)
        dX = lax.psum(dXp, 'tp').astype(jnp.bfloat16)
        return L, dW, dX

    return jax.shard_map(local, mesh=mesh,
                         in_specs=(P('dp', None), P(None, 'tp'), P('dp')),
                         out_specs=(P('dp'), P('dp', 'tp'), P('dp', None)),
                         check_vma=False)
```

profile of v0, /device:TPU:113, one launch (start us, length us, event | category | flops | bytes accessed | tf_op | source)
XLA Modules:
  0.0 1288.7 jit_solution(6938859873577502560)
XLA Ops:
  0.6 1.3 broadcast_subtract_fusion
  2.0 0.0 copy-start
  2.0 154.6 %fusion.2 = (f32[4096]{0:T(1024)S(1)}, f32[4096,4096]{0,1:T(8,128)}) fusion(bf16[4096,4096]{1,0:T(8,128)(2,1)} %param.3, bf16[4096,4096]{1,0:T(8,128)(2,1)} %param.4), kind=kOutput, calls=%fused_computation.11 | convolution fusion | flops 137455730688 | bytes 134234112 | tf_op jit(solution)/shard_map/dot_general | solution.py:12
  156.6 24.0 %pmax.7 = f32[4096]{0:T(1024)S(1)} all-reduce(f32[4096]{0:T(1024)S(1)} %get-tuple-element.10), channel_id=1, replica_groups=mesh['dp'=2,'tp'=8] {'tp'}, use_global_device_ids=true, to_apply=%region_1.0 | all-reduce | flops 4096 | bytes 32768 | tf_op jit(solution)/shard_map/pmax | solution.py:17
  180.6 0.0 copy-done
  180.6 21.7 %exponential_reduce_fusion = (f32[4096]{0:T(1024)S(1)}, f32[4096]{0:T(1024)S(1)}) fusion(f32[4096,4096]{0,1:T(8,128)} %get-tuple-element.11, f32[4096]{0:T(1024)S(1)} %get-tuple-element.10, s32[4096]{0:T(1024)S(1)} %copy-done), kind=kLoop, calls=%fused_computation.3 | loop fusion | flops 83877888 | bytes 67174400 | tf_op jit(solution)/shard_map/reduce_sum | solution.py:14
  202.4 23.9 %psum.14 = f32[2,4096]{1,0:T(2,128)S(1)} all-reduce(f32[2,4096]{1,0:T(2,128)S(1)} %pad_maximum_fusion), channel_id=1, replica_groups=mesh['dp'=2,'tp'=8] {'tp'}, use_global_device_ids=true, to_apply=%region_4.5 | all-reduce | flops 8192 | bytes 65536 | tf_op jit(solution)/shard_map/psum | solution.py:18
  226.3 0.6 subtract_reduce_fusion
  227.5 160.1 %convert_bitcast_fusion = bf16[4096,4096]{0,1:T(8,128)(2,1)} fusion(bf16[4096,4096]{1,0:T(8,128)(2,1)} %param.3, f32[4096,4096]{0,1:T(8,128)} %get-tuple-element.11, f32[4096]{0:T(1024)S(1)} %bitcast.16, f32[4096]{0:T(1024)S(1)} %pmax.7, s32[4096]{0:T(1024)S(1)} %copy-done), kind=kOutput, calls=%fused_computation.4 | convolution fusion | flops 137573171200 | bytes 134266880 | tf_op jit(solution)/shard_map/th,tv->hv/dot_general | solution.py:22
  387.7 188.7 %fusion = f32[4096,4096]{1,0:T(8,128)} fusion(bf16[4096,4096]{1,0:T(8,128)(2,1)} %param.4, f32[4096,4096]{0,1:T(8,128)} %get-tuple-element.11, f32[4096]{0:T(1024)S(1)} %bitcast.17, f32[4096]{0:T(1024)S(1)} %pmax.7, s32[4096]{0:T(1024)S(1)} %copy-done), kind=kOutput, calls=%fused_computation.9 | convolution fusion | flops 137556393984 | bytes 167821312 | tf_op jit(solution)/shard_map/tv,hv->th/dot_general | solution.py:23
  576.4 667.0 %all-reduce.1 = bf16[4096,4096]{1,0:T(8,128)(2,1)} all-reduce(f32[4096,4096]{1,0:T(8,128)} %fusion), channel_id=1, replica_groups=mesh['dp'=2,'tp'=8] {'tp'}, use_global_device_ids=true, to_apply=%region_6.7 | all-reduce | flops 16777216 | bytes 100663296 | tf_op jit(solution)/shard_map/psum | solution.py:24
  1243.4 44.1 %copy.6 = bf16[4096,4096]{1,0:T(8,128)(2,1)} copy(bf16[4096,4096]{0,1:T(8,128)(2,1)} %convert_bitcast_fusion) | data formatting | bytes 67108864
  (3 shorter events, 0.1 us)
Async XLA Ops:
  2.0 178.6 %copy-start = (s32[4096]{0:T(1024)S(1)}, s32[4096]{0:T(1024)}, u32[]{:S(2)}) copy-start(s32[4096]{0:T(1024)} %broadcast_subtract_fusion) | copy-start | bytes 49156
where the time goes:
time: 1290 us
  blocking collectives  715 us (55%)
  matrix products  503 us (39%)
  local copies, waits for them, and re-layouts  44.1 us (3%)
  other arithmetic  23.7 us (2%)
    psum x1, blocking collectives, local(): dX = lax.psum(dXp, 'tp').astype(jnp.bfloat16)  667 us
    dot_general x1, matrix products, local(): dXp = jnp.einsum('tv,hv->th', G, W, preferred_element_type=jnp.float32)  189 us
    dot_general x1, matrix products, local(): jnp.einsum('th,tv->hv', X, G, preferred_element_type=jnp.float32)  160 us
    dot_general x1, matrix products, local(): Z = jnp.dot(X, W, preferred_element_type=jnp.float32)  155 us
    unnamed x3, local copies, waits for them, and re-layouts  44.1 us

commit v1 on v0

v1 whole, which is shorter than its diff:
```python
import functools

import jax
import jax.numpy as jnp
from jax import lax
from jax.experimental import pallas as pl
from jax.experimental.pallas import tpu as pltpu
from jax.sharding import PartitionSpec as P

TB = 512
CN = 512
PERIOD = 6
OFFS = (0, 1, 2, 3, 5, 6, 8, 10)


def kernel(n, X, W, lab, Lo, dW, dX, Gh, Q, rA, rB, rC,
           wg, xb, gb, prs, st_send, st_recv, va, vq, vs, vt, ro,
           wsem, xsem, lsem, gsem, stS, stR, cred, psS, psR, qsem, xssem, odsem,
           aS, aR, bS, bR, cS, cR, gS, gR, rS, rR, sS, sR, ldsem, rosem):
    T, H = X.shape
    V = W.shape[1]
    NB, NV = T // TB, V // CN
    HH = H // 2
    ND = HH // CN
    NU = 2 * NB
    UR = TB // 2
    nc = n // 2
    QR = UR // nc
    HR = QR // 2
    f32, bf16 = jnp.float32, jnp.bfloat16
    me = lax.axis_index('tp')
    core = me % 2
    chip = me // 2
    sib = chip * 2 + 1 - core
    cn, cp, cf = (chip + 1) % nc, (chip + nc - 1) % nc, (chip + 2) % nc
    nxt, prv = cn * 2 + core, cp * 2 + core
    off = me * V

    def rcopy(src, dst, ss, rs, dev):
        return pltpu.make_async_remote_copy(src_ref=src, dst_ref=dst, send_sem=ss, recv_sem=rs,
                                            device_id={'tp': dev}, device_id_type=pl.DeviceIdType.MESH)

    def lcopy(src, dst, sem):
        return pltpu.make_async_copy(src, dst, sem)

    def mo(x, m):
        return x if isinstance(x, int) else pl.multiple_of(x, m)

    def cols(j):
        return pl.ds(mo(j * CN, CN), CN)

    def xcopy(b):
        return lcopy(X.at[pl.ds(mo(b * TB, TB), TB)], xb, xsem)

    def wcopy(j):
        return lcopy(W.at[:, cols(j)], wg.at[:, cols(j)], wsem.at[j])

    def qrows(u, c, h):
        return Q.at[pl.ds(mo(u * UR + c * QR + h * HR, HR), HR)]

    def rrows(r, d, u):
        return r.at[d, pl.ds(mo(u * HR, HR), HR)]

    def xrows(u, c, h, rows, k):
        return dX.at[pl.ds(mo(u * UR + c * QR + h * HR, HR), rows), pl.ds(mo(k * HH, HH), HH)]

    def sendA(u, d):
        return rcopy(qrows(u, cf, d), rrows(rA, d, u), aS.at[d], aR.at[d, u], (nxt, prv)[d])

    def sendB(u, d):
        return rcopy(qrows(u, (cn, cp)[d], 1 - d), rrows(rB, d, u), bS.at[d], bR.at[d, u], (nxt, prv)[d])

    def sendC(u, d):
        return rcopy(va.at[d], rrows(rC, d, u), cS.at[d], cR.at[d, u], (nxt, prv)[d])

    def loadC(u):
        return ([lcopy(rrows(rA, d, u), va.at[d], ldsem.at[d]) for d in (0, 1)]
                + [lcopy(qrows(u, (cn, cp)[d], d), vq.at[d], ldsem.at[2 + d]) for d in (0, 1)])

    def loadS(u):
        return ([lcopy(qrows(u, chip, h), vs.at[h], ldsem.at[4 + h]) for h in (0, 1)]
                + [lcopy(rrows(rC, h, u), vt.at[0, h], ldsem.at[6 + h]) for h in (0, 1)]
                + [lcopy(rrows(rB, 1 - h, u), vt.at[1, h], ldsem.at[8 + h]) for h in (0, 1)])

    def sendG(u, d):
        return rcopy(ro, xrows(u, chip, 0, QR, core), gS.at[d], gR.at[d, u], (nxt, prv)[d])

    def recvG(u, d):
        return rcopy(ro, xrows(u, (cp, cn)[d], 0, QR, core), gS.at[d], gR.at[d, u], (nxt, prv)[d])

    def sendR(u, d):
        r = xrows(u, (cp, cn)[d], d, HR, core)
        return rcopy(r, r, rS.at[d], rR.at[d, u], (nxt, prv)[d])

    def recvR(u, d):
        r = xrows(u, cf, d, HR, core)
        return rcopy(r, r, rS.at[d], rR.at[d, u], (nxt, prv)[d])

    def sibO(u):
        return rcopy(ro, xrows(u, chip, 0, QR, core), sS.at[0], sR.at[u], sib)

    def sibG(u, d):
        r = xrows(u, (cp, cn)[d], 0, QR, core)
        return rcopy(r, r, sS.at[1 + d], sR.at[u], sib)

    def sibR(u):
        r = xrows(u, cf, 0, QR, core)
        return rcopy(r, r, sS.at[3], sR.at[u], sib)

    def sibW(u):
        r = dX.at[pl.ds(mo(u * UR, UR), UR), pl.ds(mo((1 - core) * HH, HH), HH)]
        return rcopy(r, r, sS.at[0], sR.at[u], sib)

    def ownO(u):
        return lcopy(ro, xrows(u, chip, 0, QR, core), rosem)

    def st0(u):
        @pl.when(u > 0)
        def _():
            for d in (0, 1):
                sendA(u - 1, d).wait_send()
        for d in (0, 1):
            sendA(u, d).start()

    def st1(u):
        @pl.when(u > 0)
        def _():
            for d in (0, 1):
                sendB(u - 1, d).wait_send()
        for d in (0, 1):
            sendB(u, d).start()

    def st2(u):
        @pl.when(u > 0)
        def _():
            for d in (0, 1):
                sendC(u - 1, d).wait_send()
        for d in (0, 1):
            sendA(u, d).wait_recv()
        for c in loadC(u):
            c.start()

    def st3(u):
        for c in loadC(u):
            c.wait()
        va[...] = va[...] + vq[...]
        for d in (0, 1):
            sendC(u, d).start()

    def st4(u):
        for d in (0, 1):
            sendB(u, d).wait_recv()
            sendC(u, d).wait_recv()
        for c in loadS(u):
            c.start()

    def st5(u):
        @pl.when(u > 0)
        def _():
            for d in (0, 1):
                sendG(u - 1, d).wait_send()
            sibO(u - 1).wait_send()
            ownO(u - 1).wait()
        for c in loadS(u):
            c.wait()
        for h in (0, 1):
            ro[h * HR:(h + 1) * HR] = ((vt[0, h] + vs[h]) + vt[1, h]).astype(bf16)
        for d in (0, 1):
            sendG(u, d).start()
        ownO(u).start()
        sibO(u).start()

    def st6(u):
        @pl.when(u > 0)
        def _():
            for d in (0, 1):
                sendR(u - 1, d).wait_send()
                sibG(u - 1, d).wait_send()
        for d in (0, 1):
            recvG(u, d).wait_recv()
        for d in (0, 1):
            sendR(u, d).start()
        for d in (0, 1):
            sibG(u, d).start()

    def st7(u):
        @pl.when(u > 0)
        def _():
            sibR(u - 1).wait_send()
        for d in (0, 1):
            recvR(u, d).wait_recv()
        sibR(u).start()

    ST = NV // 2
    K0 = 3 * ST

    def exchange(k):
        for o, fn in reversed(tuple(zip(OFFS, (st0, st1, st2, st3, st4, st5, st6, st7)))):
            t = k - (K0 + o)
            u = t // PERIOD

            @pl.when((t >= 0) & (t % PERIOD == 0) & (u < NU))
            def _(fn=fn, u=u):
                fn(u)

    barrier = pltpu.get_barrier_semaphore()
    for i in range(1, n):
        pl.semaphore_signal(barrier, inc=1, device_id={'tp': (me + i) % n}, device_id_type=pl.DeviceIdType.MESH)
    pl.semaphore_wait(barrier, n - 1)
    xcopy(0).start()
    for j in range(NV):
        wcopy(j).start()

    def stat_copy(par, i):
        peer = (me + i) % n
        return rcopy(st_send.at[par], st_recv.at[par, me], stS.at[par, i], stR.at[par, me], peer)

    def stat_recv(par, i):
        src = (me + n - i) % n
        return rcopy(st_send.at[par], st_recv.at[par, src], stS.at[par, i], stR.at[par, src], src)

    def gcopy(b):
        return lcopy(gb, Gh.at[pl.ds(mo(b * TB, TB), TB)], gsem.at[0])

    def phase1(eb, za, zb, ps, qs, lb, m_run, s_run, z_run, mjs, lacc):
        RT = min(64, TB)
        lane = lax.broadcasted_iota(jnp.int32, (RT, 128), 1)
        laneT = lax.broadcasted_iota(jnp.int32, (TB, 128), 1)

        def lcp(b):
            return lcopy(lab.at[pl.ds(mo(b * TB, TB), TB)], lb.at[b % 2], lsem)

        lcp(0).start()
        lacc[...] = jnp.zeros_like(lacc)

        def zdot(j, z):
            z[...] = jnp.dot(xb[...], wg[:, cols(j)], preferred_element_type=f32)

        def epi(z, j, par):
            base = j * CN
            for r in range(0, TB, RT):
                rows = slice(r, r + RT)
                zq = [z[rows, q * 128:(q + 1) * 128] for q in range(CN // 128)]
                mx = functools.reduce(jnp.maximum, zq)
                m_old = m_run[rows]
                m_new = jnp.maximum(m_old, jnp.max(mx, axis=1, keepdims=True))
                m_run[rows] = m_new
                mjs[rows] = jnp.where(lane == j, m_new, mjs[rows])
                s = s_run[rows] * jnp.exp(m_old - m_new)
                t = z_run[rows]
                lb_r = lb[par, rows] - (off + base)
                for q in range(CN // 128):
                    e = jnp.exp(zq[q] - m_new)
                    eb[j, rows, q * 128:(q + 1) * 128] = e
                    s = s + e
                    t = t + jnp.where(lane + q * 128 == lb_r, zq[q], 0.0)
                s_run[rows] = s
                z_run[rows] = t

        def zphase(b):
            par = b % 2
            xcopy(b).wait()
            lcp(b).wait()
            m_run[...] = jnp.full_like(m_run, -jnp.inf)
            s_run[...] = jnp.zeros_like(s_run)
            z_run[...] = jnp.zeros_like(z_run)
            mjs[...] = jnp.zeros_like(mjs)

            def wwait(j):
                @pl.when(b == 0)
                def _():
                    wcopy(j).wait()

            wwait(0)
            zdot(0, za)

            def body(i, c):
                exchange(2 * ST * b - ST + i)
                wwait(2 * i + 1)
                wwait(2 * i + 2)
                zdot(2 * i + 1, zb)
                epi(za, 2 * i, par)
                zdot(2 * i + 2, za)
                epi(zb, 2 * i + 1, par)
                return c

            lax.fori_loop(0, NV // 2 - 1, body, 0)
            exchange(2 * ST * b - 1)
            wwait(NV - 1)
            zdot(NV - 1, zb)
            epi(za, NV - 2, par)

            @pl.when(b < NB - 1)
            def _():
                xcopy(b + 1).start()
            epi(zb, NV - 1, par)

        def send_stats(b):
            par = b % 2
            s = jnp.sum(s_run[...], axis=1, keepdims=True)
            t = jnp.sum(z_run[...], axis=1, keepdims=True)
            a = jnp.where(laneT == 0, m_run[...], jnp.where(laneT == 1, s, jnp.where(laneT == 2, t, 0.0)))
            at = a.T[0:8]

            @pl.when(b >= 2)
            def _():
                for i in range(1, n):
                    stat_copy(par, i).wait_send()
            st_send[par] = at
            st_recv[par, me] = at
            for i in range(1, n):
                stat_copy(par, i).start()

        def gpass(b):
            par = b % 2
            for i in range(1, n):
                stat_recv(par, i).wait_recv()
            ms = [st_recv[par, i, 0:1] for i in range(n)]
            M = functools.reduce(jnp.maximum, ms)
            S = sum(st_recv[par, i, 1:2] * jnp.exp(ms[i] - M) for i in range(n))
            zt = sum(st_recv[par, i, 2:3] for i in range(n))
            lacc[...] = lacc[...] + ((M + jnp.log(S)) - zt)
            sub = lax.broadcasted_iota(jnp.int32, (128, TB), 0)
            bt = jnp.where(sub == 0, M, jnp.where(sub == 1, 1.0 / S, 0.0)).T
            R = jnp.exp(mjs[...] - bt[:, 0:1]) * bt[:, 1:2]
            mjs[...] = R

            @pl.when(b > 0)
            def _():
                gcopy(b - 1).wait()

            def body(j, c):
                for r in range(0, TB, RT):
                    rows = slice(r, r + RT)
                    rj = jnp.sum(jnp.where(lane == j, mjs[rows], 0.0), axis=1, keepdims=True)
                    lb_r = lb[par, rows] - (off + j * CN)
                    for q in range(CN // 128):
                        e = eb[j, rows, q * 128:(q + 1) * 128] * rj
                        e = (e - jnp.where(lane + q * 128 == lb_r, 1.0, 0.0)) * (1.0 / T)
                        gb[rows, pl.ds(mo(j * CN + q * 128, 128), 128)] = e.astype(bf16)
                return c

            lax.fori_loop(0, NV, body, 0)
            gcopy(b).start()

        def dxdot(row0):
            return lax.dot_general(gb[...], wg[pl.ds(mo(row0, CN), CN), :], (((1,), (1,)), ((), ())),
                                   preferred_element_type=f32)

        def pscopy(j, s):
            return rcopy(ps.at[s], prs.at[j], psS.at[s], psR.at[j], sib)

        def qcopy(b, j, s):
            return lcopy(qs.at[s], Q.at[pl.ds(mo(b * TB, TB), TB), cols(j)], qsem.at[s])

        def dxphase(b, k0):
            def body_s(i, c):
                exchange(k0 + i)
                for s in (0, 1):
                    j = 2 * i + s

                    @pl.when(i > 0)
                    def _(j=j, s=s):
                        pscopy(j - 2, s).wait_send()
                    ps[s] = dxdot((1 - core) * HH + j * CN)

                    @pl.when(b > 0)
                    def _(j=j):
                        pl.semaphore_wait(cred.at[j], 1)
                    pscopy(j, s).start()
                return c

            lax.fori_loop(0, ND // 2, body_s, 0)

            def body_o(i, c):
                exchange(k0 + ND // 2 + i)
                for s in (0, 1):
                    j = 2 * i + s

                    @pl.when(i > 0)
                    def _(j=j, s=s):
                        qcopy(b, j - 2, s).wait()
                    pscopy(j, s).wait_recv()
                    qs[s] = dxdot(core * HH + j * CN) + prs[j]
                    qcopy(b, j, s).start()

                    @pl.when(b < NB - 1)
                    def _(j=j):
                        pl.semaphore_signal(cred.at[j], inc=1, device_id={'tp': sib},
                                            device_id_type=pl.DeviceIdType.MESH)
                return c

            lax.fori_loop(0, ND // 2, body_o, 0)
            for s in (0, 1):
                pscopy(ND - 2 + s, s).wait_send()

        def block(b, c):
            @pl.when(b < NB)
            def _():
                zphase(b)
                send_stats(b)

                @pl.when(b < NB - 1)
                def _():
                    lcp(b + 1).start()

            @pl.when(b == NB)
            def _():
                for i in range(T // TB):
                    x0copy(i).start()

            @pl.when(b > 0)
            def _():
                dxphase(b - 1, jnp.minimum(2 * ST * b, (2 * NB - 1) * ST))

            @pl.when(b < NB)
            def _():
                gpass(b)

            @pl.when(b > 0)
            def _():
                for s in (0, 1):
                    qcopy(b - 1, ND - 2 + s, s).wait()
            return c

        lax.fori_loop(0, NB + 1, block, 0)
        for b in (NB - 2, NB - 1):
            for i in range(1, n):
                stat_copy(b % 2, i).wait_send()
        Lo[...] = jnp.zeros_like(Lo) + jnp.sum(lacc[...], axis=1, keepdims=True) * (1.0 / T)

    def x0copy(i):
        return lcopy(X.at[pl.ds(i * TB, TB), pl.ds(0, TB)], xb.at[:, pl.ds(i * TB, TB)], wsem.at[i])

    pl.run_scoped(phase1,
                  pltpu.VMEM((NV, TB, CN), f32), pltpu.VMEM((TB, CN), f32), pltpu.VMEM((TB, CN), f32),
                  pltpu.VMEM((2, TB, CN), f32), pltpu.VMEM((2, TB, CN), f32), pltpu.VMEM((2, TB, 128), jnp.int32),
                  pltpu.VMEM((TB, 128), f32), pltpu.VMEM((TB, 128), f32), pltpu.VMEM((TB, 128), f32),
                  pltpu.VMEM((TB, 128), f32), pltpu.VMEM((1, TB), f32))

    KD = 2 * ST * NB
    NH = H // TB

    def phase2(xs, od):
        SL = T // (NV // 2)

        def gload(j):
            return lcopy(Gh.at[:, cols(j)], wg.at[:, cols(j)], gsem.at[j])

        def xscopy(h, i):
            return lcopy(X.at[pl.ds(mo(i * SL, SL), SL), pl.ds(mo(h * TB, TB), TB)], xs.at[i % 2], xssem.at[i % 2])

        def odcopy(h, j, s):
            return lcopy(od.at[s], dW.at[pl.ds(mo(h * TB, TB), TB), cols(j)], odsem.at[s])

        gcopy(NB - 1).wait()
        for j in range(NV):
            gload(j).start()
        xscopy(1, 0).start()
        for i in range(T // TB):
            x0copy(i).wait()

        def tr0(i, c):
            gb[:, pl.ds(mo(i * TB, TB), TB)] = xb[:, pl.ds(mo(i * TB, TB), TB)].T
            return c

        lax.fori_loop(0, T // TB, tr0, 0)

        def hstep(h, cur, fut):
            def body(i, c):
                exchange(KD + h * (NV // 2) + i)

                @pl.when(h == 0)
                def _():
                    gload(2 * i).wait()
                    gload(2 * i + 1).wait()

                @pl.when((h > 0) | (i > 0))
                def _():
                    for s in (0, 1):
                        odcopy(h, 2 * i + s, s).wait()
                hn = jnp.minimum(h + 1, NH - 1)
                xscopy(hn, i).wait()

                @pl.when((h < NH - 1) | (i < NV // 2 - 1))
                def _():
                    last = i == NV // 2 - 1
                    xscopy(jnp.minimum(jnp.where(last, h + 2, h + 1), NH - 1), jnp.where(last, 0, i + 1)).start()
                for s in (0, 1):
                    od[s] = jnp.dot(cur[...], wg[:, cols(2 * i + s)], preferred_element_type=f32).astype(bf16)
                fut[:, pl.ds(mo(i * SL, SL), SL)] = xs[i % 2].T
                for s in (0, 1):
                    odcopy(h, 2 * i + s, s).start()
                return c

            lax.fori_loop(0, NV // 2, body, 0)

        def hpair(hh, c):
            hstep(2 * hh, gb, xb)
            hstep(2 * hh + 1, xb, gb)
            return c

        lax.fori_loop(0, NH // 2, hpair, 0)
        for s in (0, 1):
            odcopy(NH - 1, NV - 2 + s, s).wait()

    pl.run_scoped(phase2, pltpu.VMEM((2, T // (NV // 2), TB), bf16), pltpu.VMEM((2, TB, CN), bf16))

    KE = KD + NH * (NV // 2)
    KL = K0 + OFFS[-1] + PERIOD * (NU - 1) + 1

    def tail(k, c):
        exchange(k)
        return c

    lax.fori_loop(KE, max(KL, KE), tail, 0)
    u = NU - 1
    for d in (0, 1):
        sendA(u, d).wait_send()
        sendB(u, d).wait_send()
        sendC(u, d).wait_send()
        sendG(u, d).wait_send()
        sendR(u, d).wait_send()
        sibG(u, d).wait_send()
    sibO(u).wait_send()
    sibR(u).wait_send()
    ownO(u).wait()

    def sw(u, c):
        sibW(u).wait_recv()
        return c

    lax.fori_loop(0, NU, sw, 0)


def solution(mesh):
    n = mesh.shape['tp']

    def local(X, W, labels):
        T, H = X.shape
        V = W.shape[1]
        NB, NV = T // TB, V // CN
        NU, UR = 2 * NB, TB // 2
        HH = H // 2
        QR = UR // (n // 2)
        HR = QR // 2
        lab = jnp.broadcast_to(labels[:, None], (T, 128))
        f32, bf16 = jnp.float32, jnp.bfloat16
        S = jax.ShapeDtypeStruct
        D = pltpu.SemaphoreType.DMA
        hbm = pl.BlockSpec(memory_space=pl.ANY)
        outs = pl.pallas_call(
            functools.partial(kernel, n),
            out_shape=[S((8, 128), f32), S((H, V), bf16), S((T, H), bf16), S((T, V), bf16), S((T, HH), f32),
                       S((2, NU * HR, HH), f32), S((2, NU * HR, HH), f32), S((2, NU * HR, HH), f32)],
            in_specs=[hbm] * 3,
            out_specs=[pl.BlockSpec(memory_space=pltpu.VMEM)] + [hbm] * 7,
            scratch_shapes=[
                pltpu.VMEM((H, V), bf16), pltpu.VMEM((TB, H), bf16), pltpu.VMEM((TB, V), bf16),
                pltpu.VMEM((HH // CN, TB, CN), f32),
                pltpu.VMEM((2, 8, TB), f32), pltpu.VMEM((2, n, 8, TB), f32),
                pltpu.VMEM((2, HR, HH), f32), pltpu.VMEM((2, HR, HH), f32), pltpu.VMEM((2, HR, HH), f32),
                pltpu.VMEM((2, 2, HR, HH), f32), pltpu.VMEM((QR, HH), bf16),
                D((NV,)), D, D, D((NV,)), D((2, n)), D((2, n)), pltpu.SemaphoreType.REGULAR((HH // CN,)),
                D((2,)), D((HH // CN,)), D((2,)), D((2,)), D((2,)),
                D((2,)), D((2, NU)), D((2,)), D((2, NU)), D((2,)), D((2, NU)), D((2,)), D((2, NU)),
                D((2,)), D((2, NU)), D((4,)), D((NU,)), D((10,)), D,
            ],
            compiler_params=pltpu.CompilerParams(collective_id=0, has_side_effects=True,
                                                 vmem_limit_bytes=67043328),
            cost_estimate=pl.CostEstimate(flops=6 * T * H * V, bytes_accessed=8 * T * H, transcendentals=T * V),
        )(X, W, lab)
        return outs[0][0, :1], outs[1], outs[2]

    return jax.shard_map(local, mesh=mesh,
                         in_specs=(P('dp', None), P(None, 'tp'), P('dp')),
                         out_specs=(P('dp'), P('dp', 'tp'), P('dp', None)),
                         check_vma=False)
```

time: 1290 us -> 704 us (0.55)
  blocking collectives: 715 us -> 0 us
  Pallas kernels: 0 us -> 652 us
  matrix products: 503 us -> 0 us
  other arithmetic: 23.7 us -> 0 us
    psum x2 -> x0, blocking collectives: 691 us -> none  [the longest x1 667 us: local(): dX = lax.psum(dXp, 'tp').astype(jnp.bfloat16)]
    pallas_call x0 -> x1, Pallas kernels: none -> 652 us  [local(): pl.pallas_call(functools.partial(kernel, n), out_shape=[S((8, 128), f32),...]
    dot_general x3 -> x0, matrix products: 503 us -> none  [the longest x1 189 us: local(): dXp = jnp.einsum('tv,hv->th', G, W, preferred_element_type=jnp.float32)]
    pmax x1 -> x0, blocking collectives: 24 us -> none  [local(): M = lax.pmax(m, 'tp')]
    reduce_sum x2 -> x0, other arithmetic: 22.4 us -> none  [the longest x1 21.7 us: local(): s = jnp.exp(Z - m[:, None]).sum(axis=1)]
    unnamed x3 -> x2, local copies, waits for them, and re-layouts: 44.1 us -> 45.8 us
where the time goes in v1:
time: 704 us; the launch traced here: 703 us
  Pallas kernels  652 us (93%)
  local copies, waits for them, and re-layouts  50.4 us (7%)
    pallas_call x1, Pallas kernels, local(): pl.pallas_call(functools.partial(kernel, n), out_shape=[S((8, 128), f32),...  652 us
    unnamed x2, local copies, waits for them, and re-layouts  45.8 us

profile of v1, /device:TPU:113, one launch (start us, length us, event | category | flops | bytes accessed | tf_op | source)
XLA Modules:
  0.0 703.5 jit_solution(11706968968894863397)
XLA Ops:
  0.6 3.4 broadcast_in_dim.2.lab
  4.1 652.4 %shard_map.58 = (f32[8,128]{1,0:T(8,128)}, bf16[4096,4096]{1,0:T(8,128)(2,1)}, bf16[4096,4096]{1,0:T(8,128)(2,1)}, bf16[4096,4096]{1,0:T(8,128)(2,1)}, f32[4096,...) custom-call(bf16[4096,4096]{1,0:T(8,128)(2,1)} %X.1, ...), custom_call_target="tpu_custom_call" | custom-call | flops 412316860416 | bytes 134217728 | tf_op jit(solution)/shard_map/pallas_call | solution.py:552
  656.5 1.2 slice.3
  657.7 22.9 %copy.8 = bf16[4096,4096]{1,0:T(8,128)(2,1)} copy(bf16[4096,4096]{1,0:T(8,128)(2,1)} %get-tuple-element.13) | data formatting | bytes 67108864
  680.6 22.9 %copy.9 = bf16[4096,4096]{1,0:T(8,128)(2,1)} copy(bf16[4096,4096]{1,0:T(8,128)(2,1)} %get-tuple-element.14) | data formatting | bytes 67108864

commit v2 on v1

--- a/solution.py
+++ b/solution.py
@@ -9,8 +9,9 @@
 
 TB = 512
 CN = 512
-PERIOD = 6
-OFFS = (0, 1, 2, 3, 5, 6, 8, 10)
+REST = 2
+PERIOD = 5
+OFFS = (0, 1, 2, 3, 6, 7, 9, 11)
 
 
 def kernel(n, X, W, lab, Lo, dW, dX, Gh, Q, rA, rB, rC,
@@ -356,37 +357,42 @@
         def dxphase(b, k0):
             def body_s(i, c):
                 exchange(k0 + i)
-                for s in (0, 1):
-                    j = 2 * i + s
-
-                    @pl.when(i > 0)
-                    def _(j=j, s=s):
-                        pscopy(j - 2, s).wait_send()
-                    ps[s] = dxdot((1 - core) * HH + j * CN)
-
-                    @pl.when(b > 0)
-                    def _(j=j):
-                        pl.semaphore_wait(cred.at[j], 1)
-                    pscopy(j, s).start()
+
+                @pl.when(i > 0)
+                def _():
+                    for s in (0, 1):
+                        pscopy(2 * i - 2 + s, s).wait_send()
+
+                @pl.when(b > 0)
+                def _():
+                    for s in (0, 1):
+                        pl.semaphore_wait(cred.at[2 * i + s], 1)
+                for s in (0, 1):
+                    ps[s] = dxdot((1 - core) * HH + (2 * i + s) * CN)
+                for s in (0, 1):
+                    pscopy(2 * i + s, s).start()
                 return c
 
             lax.fori_loop(0, ND // 2, body_s, 0)
 
             def body_o(i, c):
                 exchange(k0 + ND // 2 + i)
-                for s in (0, 1):
-                    j = 2 * i + s
-
-                    @pl.when(i > 0)
-                    def _(j=j, s=s):
-                        qcopy(b, j - 2, s).wait()
-                    pscopy(j, s).wait_recv()
-                    qs[s] = dxdot(core * HH + j * CN) + prs[j]
-                    qcopy(b, j, s).start()
-
-                    @pl.when(b < NB - 1)
-                    def _(j=j):
-                        pl.semaphore_signal(cred.at[j], inc=1, device_id={'tp': sib},
+
+                @pl.when(i > 0)
+                def _():
+                    for s in (0, 1):
+                        qcopy(b, 2 * i - 2 + s, s).wait()
+                for s in (0, 1):
+                    pscopy(2 * i + s, s).wait_recv()
+                for s in (0, 1):
+                    qs[s] = dxdot(core * HH + (2 * i + s) * CN) + prs[2 * i + s]
+                for s in (0, 1):
+                    qcopy(b, 2 * i + s, s).start()
+
+                @pl.when(b < NB - 1)
+                def _():
+                    for s in (0, 1):
+                        pl.semaphore_signal(cred.at[2 * i + s], inc=1, device_id={'tp': sib},
                                             device_id_type=pl.DeviceIdType.MESH)
                 return c
 
@@ -439,7 +445,7 @@
                   pltpu.VMEM((TB, 128), f32), pltpu.VMEM((1, TB), f32))
 
     KD = 2 * ST * NB
-    NH = H // TB
+    NH = H // TB - REST
 
     def phase2(xs, od):
         SL = T // (NV // 2)
@@ -531,6 +537,115 @@
         return c
 
     lax.fori_loop(0, NU, sw, 0)
+
+
+def rest(X, Gh, dWa, dXa, dW, dXo, wg, xa, xb, xs, od, cx, cw, gsem, x0sem, xssem, odsem, cxsem, cwsem):
+    T, H = X.shape
+    V = Gh.shape[1]
+    NV = V // CN
+    ST = NV // 2
+    NH = H // TB
+    H0 = NH - REST
+    SL = T // ST
+    NS = REST * ST
+    f32, bf16 = jnp.float32, jnp.bfloat16
+    mo = pl.multiple_of
+    RX, RW = T // NS, H0 * TB // NS
+
+    def lcopy(src, dst, sem):
+        return pltpu.make_async_copy(src, dst, sem)
+
+    def cols(j):
+        return pl.ds(mo(j * CN, CN), CN)
+
+    def gload(j):
+        return lcopy(Gh.at[:, cols(j)], wg.at[:, cols(j)], gsem.at[j])
+
+    def x0copy(i):
+        return lcopy(X.at[pl.ds(i * TB, TB), pl.ds(H0 * TB, TB)], xb.at[:, pl.ds(i * TB, TB)], x0sem.at[i])
+
+    def xscopy(h, i):
+        return lcopy(X.at[pl.ds(mo(i * SL, SL), SL), pl.ds(mo(h * TB, TB), TB)], xs.at[i % 2], xssem.at[i % 2])
+
+    def odcopy(h, j, s):
+        return lcopy(od.at[s], dW.at[pl.ds(h * TB, TB), cols(j)], odsem.at[s])
+
+    def cin(c):
+        return (lcopy(dXa.at[pl.ds(mo(c * RX, RX), RX)], cx.at[c % 2], cxsem.at[0, c % 2]),
+                lcopy(dWa.at[pl.ds(mo(c * RW, RW), RW)], cw.at[c % 2], cwsem.at[0, c % 2]))
+
+    def cout(c):
+        return (lcopy(cx.at[c % 2], dXo.at[pl.ds(mo(c * RX, RX), RX)], cxsem.at[1, c % 2]),
+                lcopy(cw.at[c % 2], dW.at[pl.ds(mo(c * RW, RW), RW)], cwsem.at[1, c % 2]))
+
+    for i in range(T // TB):
+        x0copy(i).start()
+    for j in (0, 1):
+        gload(j).start()
+    xscopy(H0 + 1, 0).start()
+    for x in cin(0):
+        x.start()
+    for j in range(2, NV):
+        gload(j).start()
+    for i in range(T // TB):
+        x0copy(i).wait()
+
+    def tr0(i, c):
+        xa[:, pl.ds(mo(i * TB, TB), TB)] = xb[:, pl.ds(mo(i * TB, TB), TB)].T
+        return c
+
+    lax.fori_loop(0, T // TB, tr0, 0)
+
+    def hstep(r, cur, fut):
+        h = H0 + r
+
+        def body(i, c):
+            q = r * ST + i
+
+            @pl.when(q > 0)
+            def _():
+                for x in cout(q - 1):
+                    x.wait()
+
+            @pl.when(q < NS - 1)
+            def _():
+                for x in cin(q + 1):
+                    x.start()
+            for x in cin(q):
+                x.wait()
+            for x in cout(q):
+                x.start()
+            if r == 0:
+                gload(2 * i).wait()
+                gload(2 * i + 1).wait()
+            if r < REST - 1:
+                xscopy(h + 1, i).wait()
+
+                @pl.when((i < ST - 1) | (r < REST - 2))
+                def _():
+                    last = i == ST - 1
+                    xscopy(jnp.where(last, h + 2, h + 1), jnp.where(last, 0, i + 1)).start()
+
+            @pl.when(q > 0)
+            def _():
+                for s in (0, 1):
+                    odcopy(h, 2 * i + s, s).wait()
+            for s in (0, 1):
+                od[s] = jnp.dot(cur[...], wg[:, cols(2 * i + s)], preferred_element_type=f32).astype(bf16)
+            if r < REST - 1:
+                fut[:, pl.ds(mo(i * SL, SL), SL)] = xs[i % 2].T
+            for s in (0, 1):
+                odcopy(h, 2 * i + s, s).start()
+            return c
+
+        lax.fori_loop(0, ST, body, 0)
+
+    for r in range(REST):
+        hstep(r, (xa, xb)[r % 2], (xb, xa)[r % 2])
+    for s in (0, 1):
+        odcopy(NH - 1, NV - 2 + s, s).wait()
+    for x in cout(NS - 1):
+        x.wait()
 
 
 def solution(mesh):
@@ -551,7 +666,7 @@
         hbm = pl.BlockSpec(memory_space=pl.ANY)
         outs = pl.pallas_call(
             functools.partial(kernel, n),
-            out_shape=[S((8, 128), f32), S((H, V), bf16), S((T, H), bf16), S((T, V), bf16), S((T, HH), f32),
+            out_shape=[S((8, 128), f32), S((H - REST * TB, V), bf16), S((T, H), bf16), S((T, V), bf16), S((T, HH), f32),
                        S((2, NU * HR, HH), f32), S((2, NU * HR, HH), f32), S((2, NU * HR, HH), f32)],
             in_specs=[hbm] * 3,
             out_specs=[pl.BlockSpec(memory_space=pltpu.VMEM)] + [hbm] * 7,
@@ -570,7 +685,23 @@
                                                  vmem_limit_bytes=67043328),
             cost_estimate=pl.CostEstimate(flops=6 * T * H * V, bytes_accessed=8 * T * H, transcendentals=T * V),
         )(X, W, lab)
-        return outs[0][0, :1], outs[1], outs[2]
+        ST = NV // 2
+        NS = REST * ST
+        dW, dX = pl.pallas_call(
+            rest,
+            out_shape=[S((H, V), bf16), S((T, H), bf16)],
+            in_specs=[hbm] * 4,
+            out_specs=[hbm] * 2,
+            scratch_shapes=[
+                pltpu.VMEM((T, V), bf16), pltpu.VMEM((TB, T), bf16), pltpu.VMEM((TB, T), bf16),
+                pltpu.VMEM((2, T // ST, TB), bf16), pltpu.VMEM((2, TB, CN), bf16),
+                pltpu.VMEM((2, T // NS, H), bf16), pltpu.VMEM((2, (H - REST * TB) // NS, V), bf16),
+                D((NV,)), D((T // TB,)), D((2,)), D((2,)), D((2, 2)), D((2, 2)),
+            ],
+            compiler_params=pltpu.CompilerParams(vmem_limit_bytes=67043328),
+            cost_estimate=pl.CostEstimate(flops=2 * T * REST * TB * V, bytes_accessed=10 * T * H, transcendentals=0),
+        )(X, outs[3], outs[1], outs[2])
+        return outs[0][0, :1], dW, dX
 
     return jax.shard_map(local, mesh=mesh,
                          in_specs=(P('dp', None), P(None, 'tp'), P('dp')),

time: 704 us -> 654 us (0.929)
  local copies, waits for them, and re-layouts: 50.4 us -> 4.63 us
    pallas_call x1, Pallas kernels: 652 us -> 590 us  [local(): pl.pallas_call(functools.partial(kernel, n), out_shape=[S((8, 128), f32),...]
    pallas_call x0 -> x1, Pallas kernels: none -> 58.6 us  [local(): pl.pallas_call(rest, out_shape=[S((H, V), bf16), S((T, H), bf16)], in_spe...]
    unnamed x2 -> x0, local copies, waits for them, and re-layouts: 45.8 us -> none
where the time goes in v2:
time: 654 us
  Pallas kernels  648 us (99%)
    pallas_call x1, Pallas kernels, local(): pl.pallas_call(functools.partial(kernel, n), out_shape=[S((8, 128), f32),...  590 us
    pallas_call x1, Pallas kernels, local(): pl.pallas_call(rest, out_shape=[S((H, V), bf16), S((T, H), bf16)], in_spe...  58.6 us

profile of v2, /device:TPU:113, one launch (start us, length us, event | category | flops | bytes accessed | tf_op | source)
XLA Modules:
  0.0 653.7 jit_solution(9665979669433006593)
XLA Ops:
  0.6 3.4 broadcast_in_dim.2.lab
  4.1 589.7 %shard_map.58 = (f32[8,128]{1,0:T(8,128)}, bf16[3072,4096]{1,0:T(8,128)(2,1)}, bf16[4096,4096]{1,0:T(8,128)(2,1)}, bf16[4096,4096]{1,0:T(8,128)(2,1)}, f32[4096,...) custom-call(bf16[4096,4096]{1,0:T(8,128)(2,1)} %X.3, ...), custom_call_target="tpu_custom_call" | custom-call | flops 412316860416 | bytes 134217728 | tf_op jit(solution)/shard_map/pallas_call | solution.py:667
  593.7 1.2 slice.3
  594.9 58.6 %shard_map.59 = (bf16[4096,4096]{1,0:T(8,128)(2,1)}, bf16[4096,4096]{1,0:T(8,128)(2,1)}) custom-call(bf16[4096,4096]{1,0:T(8,128)(2,1)} %X.3, bf16[4096,4096]{1,0:T(8,128)(2,1)} %get-tuple-element.10.Gh, bf16[3072,4096]{1,0:T(8,128)(2,1)} %get-tuple-element.11.dWa, bf16[4096,4096]{1,0:T(8,128)(2,1)} %get-tuple-element.12.dXa), custom_call_target="tpu_custom_call" | custom-call | flops 34359738368 | bytes 167772160 | tf_op jit(solution)/shard_map/pallas_call | solution.py:690

commit v3 on v2

--- a/solution.py
+++ b/solution.py
@@ -7,6 +7,7 @@
 from jax.experimental.pallas import tpu as pltpu
 from jax.sharding import PartitionSpec as P
 
+PAIR = tuple(range(2))
 TB = 512
 CN = 512
 REST = 2
@@ -75,13 +76,13 @@
         return rcopy(va.at[d], rrows(rC, d, u), cS.at[d], cR.at[d, u], (nxt, prv)[d])
 
     def loadC(u):
-        return ([lcopy(rrows(rA, d, u), va.at[d], ldsem.at[d]) for d in (0, 1)]
-                + [lcopy(qrows(u, (cn, cp)[d], d), vq.at[d], ldsem.at[2 + d]) for d in (0, 1)])
+        return ([lcopy(rrows(rA, d, u), va.at[d], ldsem.at[d]) for d in PAIR]
+                + [lcopy(qrows(u, (cn, cp)[d], d), vq.at[d], ldsem.at[2 + d]) for d in PAIR])
 
     def loadS(u):
-        return ([lcopy(qrows(u, chip, h), vs.at[h], ldsem.at[4 + h]) for h in (0, 1)]
-                + [lcopy(rrows(rC, h, u), vt.at[0, h], ldsem.at[6 + h]) for h in (0, 1)]
-                + [lcopy(rrows(rB, 1 - h, u), vt.at[1, h], ldsem.at[8 + h]) for h in (0, 1)])
+        return ([lcopy(qrows(u, chip, h), vs.at[h], ldsem.at[4 + h]) for h in PAIR]
+                + [lcopy(rrows(rC, h, u), vt.at[0, h], ldsem.at[6 + h]) for h in PAIR]
+                + [lcopy(rrows(rB, 1 - h, u), vt.at[1, h], ldsem.at[8 + h]) for h in PAIR])
 
     def sendG(u, d):
         return rcopy(ro, xrows(u, chip, 0, QR, core), gS.at[d], gR.at[d, u], (nxt, prv)[d])
@@ -118,25 +119,25 @@
     def st0(u):
         @pl.when(u > 0)
         def _():
-            for d in (0, 1):
+            for d in PAIR:
                 sendA(u - 1, d).wait_send()
-        for d in (0, 1):
+        for d in PAIR:
             sendA(u, d).start()
 
     def st1(u):
         @pl.when(u > 0)
         def _():
-            for d in (0, 1):
+            for d in PAIR:
                 sendB(u - 1, d).wait_send()
-        for d in (0, 1):
+        for d in PAIR:
             sendB(u, d).start()
 
     def st2(u):
         @pl.when(u > 0)
         def _():
-            for d in (0, 1):
+            for d in PAIR:
                 sendC(u - 1, d).wait_send()
-        for d in (0, 1):
+        for d in PAIR:
             sendA(u, d).wait_recv()
         for c in loadC(u):
             c.start()
@@ -145,11 +146,11 @@
         for c in loadC(u):
             c.wait()
         va[...] = va[...] + vq[...]
-        for d in (0, 1):
+        for d in PAIR:
             sendC(u, d).start()
 
     def st4(u):
-        for d in (0, 1):
+        for d in PAIR:
             sendB(u, d).wait_recv()
             sendC(u, d).wait_recv()
         for c in loadS(u):
@@ -158,15 +159,15 @@
     def st5(u):
         @pl.when(u > 0)
         def _():
-            for d in (0, 1):
+            for d in PAIR:
                 sendG(u - 1, d).wait_send()
             sibO(u - 1).wait_send()
             ownO(u - 1).wait()
         for c in loadS(u):
             c.wait()
-        for h in (0, 1):
+        for h in PAIR:
             ro[h * HR:(h + 1) * HR] = ((vt[0, h] + vs[h]) + vt[1, h]).astype(bf16)
-        for d in (0, 1):
+        for d in PAIR:
             sendG(u, d).start()
         ownO(u).start()
         sibO(u).start()
@@ -174,21 +175,21 @@
     def st6(u):
         @pl.when(u > 0)
         def _():
-            for d in (0, 1):
+            for d in PAIR:
                 sendR(u - 1, d).wait_send()
                 sibG(u - 1, d).wait_send()
-        for d in (0, 1):
+        for d in PAIR:
             recvG(u, d).wait_recv()
-        for d in (0, 1):
+        for d in PAIR:
             sendR(u, d).start()
-        for d in (0, 1):
+        for d in PAIR:
             sibG(u, d).start()
 
     def st7(u):
         @pl.when(u > 0)
         def _():
             sibR(u - 1).wait_send()
-        for d in (0, 1):
+        for d in PAIR:
             recvR(u, d).wait_recv()
         sibR(u).start()
 
@@ -196,11 +197,12 @@
     K0 = 3 * ST
 
     def exchange(k):
+        t = jnp.asarray(k + K0 * PERIOD - K0, jnp.int32)
+        q, r = lax.div(t, PERIOD) - K0, lax.rem(t, PERIOD)
         for o, fn in reversed(tuple(zip(OFFS, (st0, st1, st2, st3, st4, st5, st6, st7)))):
-            t = k - (K0 + o)
-            u = t // PERIOD
-
-            @pl.when((t >= 0) & (t % PERIOD == 0) & (u < NU))
+            u = q - o // PERIOD
+
+            @pl.when((r == o % PERIOD) & (u >= 0) & (u < NU))
             def _(fn=fn, u=u):
                 fn(u)
 
@@ -360,16 +362,16 @@
 
                 @pl.when(i > 0)
                 def _():
-                    for s in (0, 1):
+                    for s in PAIR:
                         pscopy(2 * i - 2 + s, s).wait_send()
 
                 @pl.when(b > 0)
                 def _():
-                    for s in (0, 1):
+                    for s in PAIR:
                         pl.semaphore_wait(cred.at[2 * i + s], 1)
-                for s in (0, 1):
+                for s in PAIR:
                     ps[s] = dxdot((1 - core) * HH + (2 * i + s) * CN)
-                for s in (0, 1):
+                for s in PAIR:
                     pscopy(2 * i + s, s).start()
                 return c
 
@@ -380,24 +382,24 @@
 
                 @pl.when(i > 0)
                 def _():
-                    for s in (0, 1):
+                    for s in PAIR:
                         qcopy(b, 2 * i - 2 + s, s).wait()
-                for s in (0, 1):
+                for s in PAIR:
                     pscopy(2 * i + s, s).wait_recv()
-                for s in (0, 1):
+                for s in PAIR:
                     qs[s] = dxdot(core * HH + (2 * i + s) * CN) + prs[2 * i + s]
-                for s in (0, 1):
+                for s in PAIR:
                     qcopy(b, 2 * i + s, s).start()
 
                 @pl.when(b < NB - 1)
                 def _():
-                    for s in (0, 1):
+                    for s in PAIR:
                         pl.semaphore_signal(cred.at[2 * i + s], inc=1, device_id={'tp': sib},
                                             device_id_type=pl.DeviceIdType.MESH)
                 return c
 
             lax.fori_loop(0, ND // 2, body_o, 0)
-            for s in (0, 1):
+            for s in PAIR:
                 pscopy(ND - 2 + s, s).wait_send()
 
         def block(b, c):
@@ -425,7 +427,7 @@
 
             @pl.when(b > 0)
             def _():
-                for s in (0, 1):
+                for s in PAIR:
                     qcopy(b - 1, ND - 2 + s, s).wait()
             return c
 
@@ -483,7 +485,7 @@
 
                 @pl.when((h > 0) | (i > 0))
                 def _():
-                    for s in (0, 1):
+                    for s in PAIR:
                         odcopy(h, 2 * i + s, s).wait()
                 hn = jnp.minimum(h + 1, NH - 1)
                 xscopy(hn, i).wait()
@@ -492,10 +494,10 @@
                 def _():
                     last = i == NV // 2 - 1
                     xscopy(jnp.minimum(jnp.where(last, h + 2, h + 1), NH - 1), jnp.where(last, 0, i + 1)).start()
-                for s in (0, 1):
+                for s in PAIR:
                     od[s] = jnp.dot(cur[...], wg[:, cols(2 * i + s)], preferred_element_type=f32).astype(bf16)
                 fut[:, pl.ds(mo(i * SL, SL), SL)] = xs[i % 2].T
-                for s in (0, 1):
+                for s in PAIR:
                     odcopy(h, 2 * i + s, s).start()
                 return c
 
@@ -507,7 +509,7 @@
             return c
 
         lax.fori_loop(0, NH // 2, hpair, 0)
-        for s in (0, 1):
+        for s in PAIR:
             odcopy(NH - 1, NV - 2 + s, s).wait()
 
     pl.run_scoped(phase2, pltpu.VMEM((2, T // (NV // 2), TB), bf16), pltpu.VMEM((2, TB, CN), bf16))
@@ -521,7 +523,7 @@
 
     lax.fori_loop(KE, max(KL, KE), tail, 0)
     u = NU - 1
-    for d in (0, 1):
+    for d in PAIR:
         sendA(u, d).wait_send()
         sendB(u, d).wait_send()
         sendC(u, d).wait_send()
@@ -580,7 +582,7 @@
 
     for i in range(T // TB):
         x0copy(i).start()
-    for j in (0, 1):
+    for j in PAIR:
         gload(j).start()
     xscopy(H0 + 1, 0).start()
     for x in cin(0):
@@ -628,13 +630,13 @@
 
             @pl.when(q > 0)
             def _():
-                for s in (0, 1):
+                for s in PAIR:
                     odcopy(h, 2 * i + s, s).wait()
-            for s in (0, 1):
+            for s in PAIR:
                 od[s] = jnp.dot(cur[...], wg[:, cols(2 * i + s)], preferred_element_type=f32).astype(bf16)
             if r < REST - 1:
                 fut[:, pl.ds(mo(i * SL, SL), SL)] = xs[i % 2].T
-            for s in (0, 1):
+            for s in PAIR:
                 odcopy(h, 2 * i + s, s).start()
             return c
 
@@ -642,7 +644,7 @@
 
     for r in range(REST):
         hstep(r, (xa, xb)[r % 2], (xb, xa)[r % 2])
-    for s in (0, 1):
+    for s in PAIR:
         odcopy(NH - 1, NV - 2 + s, s).wait()
     for x in cout(NS - 1):
         x.wait()

time: 654 us -> 650 us (level)
  no operation moved by 1% of the time
where the time goes in v3:
time: 650 us; the launch traced here: 649 us
  Pallas kernels  644 us (99%)
    pallas_call x1, Pallas kernels, local(): pl.pallas_call(functools.partial(kernel, n), out_shape=[S((8, 128), f32),...  585 us
    pallas_call x1, Pallas kernels, local(): pl.pallas_call(rest, out_shape=[S((H, V), bf16), S((T, H), bf16)], in_spe...  58.6 us

profile of v3, /device:TPU:113, one launch (start us, length us, event | category | flops | bytes accessed | tf_op | source)
XLA Modules:
  0.0 649.3 jit_solution(2750862503270498968)
XLA Ops:
  0.6 3.4 broadcast_in_dim.2.lab
  4.1 585.3 %shard_map.58 = (f32[8,128]{1,0:T(8,128)}, bf16[3072,4096]{1,0:T(8,128)(2,1)}, bf16[4096,4096]{1,0:T(8,128)(2,1)}, bf16[4096,4096]{1,0:T(8,128)(2,1)}, f32[4096,...) custom-call(bf16[4096,4096]{1,0:T(8,128)(2,1)} %X.3, ...), custom_call_target="tpu_custom_call" | custom-call | flops 412316860416 | bytes 134217728 | tf_op jit(solution)/shard_map/pallas_call | solution.py:669
  589.4 1.2 slice.3
  590.6 58.6 %shard_map.59 = (bf16[4096,4096]{1,0:T(8,128)(2,1)}, bf16[4096,4096]{1,0:T(8,128)(2,1)}) custom-call(bf16[4096,4096]{1,0:T(8,128)(2,1)} %X.3, bf16[4096,4096]{1,0:T(8,128)(2,1)} %get-tuple-element.10.Gh, bf16[3072,4096]{1,0:T(8,128)(2,1)} %get-tuple-element.11.dWa, bf16[4096,4096]{1,0:T(8,128)(2,1)} %get-tuple-element.12.dXa), custom_call_target="tpu_custom_call" | custom-call | flops 34359738368 | bytes 167772160 | tf_op jit(solution)/shard_map/pallas_call | solution.py:692
